TPU v7x, 512 devices: a whole 4x8x8 slice. The times are simulated.
512 devices in a mesh: shot: 64 (over x, y, core), det: 8 (over z).
Axes of the slice: x: 4, y: 8, z: 8, core: 2. Of those that a mesh axis runs over, the one named last changes fastest.
Arguments:
- events: int32 [65536, 8192], P('shot', 'det'), may hold values from 0 to 1, as said below
- pair_patches: int32 [8, 26, 2], P('det'), may hold values from 0 to 7, as said below
- pair_owners: int32 [8, 26, 2], P('det'), may hold values from 0 to 63, as said below
- triples: int32 [8, 256, 3], P('det'), may hold values from 0 to 1023, as said below
Outputs:
- intra_rates: float32 [64, 128, 128], P('det', 'shot')
- boundary_rates: float32 [8, 64, 2, 128, 128], P('det', 'shot')
- detector_load: float32 [64, 128], P(None, 'shot')
- triple_cumulant: float32 [8, 256], P('det')
Inputs may be any that keep to these rules, and one draw needn't show every extreme that they name: events[s, i] is 1 where detector i fired in shot s, else 0. `pair_patches`: row d lists 26 blocks of panel d, each naming two different patches of the panel; no two blocks name the same two patches. `pair_owners`: of the 52 owner entries of one panel, no shot index is named more than 2 times, and in every panel some index is named exactly 2 times. `triples`: each triple holds three different detector indices of the panel in increasing order.
All inputs are finite; a program needn't handle non-finite values.
Results may differ from a plain program's by a relative error of at most 0.0003.
Values sent between devices are 32-bit elements; how exact they have to be, the bound alone decides.
No kernel may reach another device: no remote copies, remote signals or barrier semaphores. Data moves between devices by JAX's collectives and lax.ppermute only.
A program may use at most 64 MiB of HBM per device.

v0:
```python
import jax
import jax.numpy as jnp
from jax import lax
from jax.sharding import Mesh
from jax.sharding import PartitionSpec as P

PB = 128
SHOT = ("shot_0", "shot_1", "shot_2")


def split_up(x, dim, count):
    before, after = (x.shape[:dim], x.shape[dim + 1 :])
    return jnp.moveaxis(x.reshape(*before, count, -1, *after), dim, 0)


def sum_at_owner(x, axis, dim):
    tiles = split_up(x, dim, lax.axis_size(axis))
    arrived = lax.all_to_all(tiles, axis, split_axis=0, concat_axis=0, tiled=True)
    return arrived.sum(axis=0)


def by_axis(x, axes):
    for axis in axes:
        x = lax.psum(x, axis)
    return x


def laid_out(tiles, dim):
    tiles = jnp.moveaxis(tiles, 0, dim)
    dims = tiles.shape
    return tiles.reshape(*dims[:dim], dims[dim] * dims[dim + 1], *dims[dim + 2 :])


def sent_to_all(x, axis):
    copies = jnp.broadcast_to(x, (lax.axis_size(axis), *x.shape))
    return lax.all_to_all(copies, axis, split_axis=0, concat_axis=0, tiled=True)


def gather_directly(x, axis, dim):
    return laid_out(sent_to_all(x, axis), dim)


def fit_rates(coincide, row_count, col_count, shot_total):
    inverse = 1.0 / shot_total
    joint_rate = coincide * inverse
    row_rate = row_count[..., :, None] * inverse
    col_rate = col_count[..., None, :] * inverse
    denominator = jnp.maximum(1.0 - 2.0 * row_rate - 2.0 * col_rate + 4.0 * joint_rate, 0.25)
    excess = (joint_rate - row_rate * col_rate) / denominator
    return 100.0 * (0.5 - 0.5 * jnp.sqrt(jnp.maximum(1.0 - 4.0 * excess, 0.04)))


def route_table(owner_row, shot_count, recv_slots):
    owner_ids = jnp.arange(shot_count, dtype=jnp.int32)
    hit = owner_row[None, :] == owner_ids[:, None]
    rank = jnp.cumsum(hit.astype(jnp.int32), axis=1) - 1
    slot_ids = jnp.arange(recv_slots, dtype=jnp.int32)
    chosen = hit[:, None, :] & (rank[:, None, :] == slot_ids[None, :, None])
    entry_pair = jnp.arange(owner_row.shape[0], dtype=jnp.int32) // 2
    pair_slot = jnp.sum(jnp.where(chosen, entry_pair[None, None, :], 0), axis=2)
    valid = jnp.any(chosen, axis=2).astype(jnp.float32)
    return (pair_slot, valid)


def local(events, pair_patches, pair_owners, triples):
    shot_dev, det_dev = events.shape
    shot_count = lax.axis_size(SHOT)
    shot_index = lax.axis_index(SHOT)
    shot_total = float(shot_dev * shot_count)
    inverse = 1.0 / shot_total
    patch_dev = det_dev // PB
    rows_own = PB // shot_count
    pair_count = pair_patches.shape[1]
    triple_count = triples.shape[1]
    recv_slots = max(2, 4 * pair_count // shot_count)
    bit_matrix = events.astype(jnp.bfloat16)
    patches = bit_matrix.reshape(shot_dev, patch_dev, PB)
    local_counts = jnp.sum(events, axis=0).astype(jnp.float32)
    triple_index = triples[0]
    picked = (
        jnp.take(events, triple_index.reshape(-1), axis=1)
        .astype(jnp.float32)
        .reshape(shot_dev, triple_count, 3)
    )
    first_bit = picked[:, :, 0]
    second_bit = picked[:, :, 1]
    third_bit = picked[:, :, 2]
    triple_terms = jnp.stack(
        [
            jnp.sum(first_bit * second_bit, axis=0),
            jnp.sum(first_bit * third_bit, axis=0),
            jnp.sum(second_bit * third_bit, axis=0),
            jnp.sum(first_bit * second_bit * third_bit, axis=0),
        ]
    )
    intra = jnp.einsum("sai,saj->aij", patches, patches, preferred_element_type=jnp.float32)
    pair_ends = pair_patches[0]
    first_columns = jnp.take(patches, pair_ends[:, 0], axis=1)
    second_columns = jnp.take(patches, pair_ends[:, 1], axis=1)
    cross = jnp.einsum(
        "spi,spj->pij", first_columns, second_columns, preferred_element_type=jnp.float32
    )
    joined = sum_at_owner(jnp.concatenate([intra, cross], axis=0), SHOT, 1)
    intra_share = joined[:patch_dev]
    pair_share = joined[patch_dev:]
    counts, triple_total = (by_axis(local_counts, SHOT), by_axis(triple_terms, SHOT))
    patch_counts = counts.reshape(patch_dev, PB)
    row_counts = lax.dynamic_slice_in_dim(patch_counts, shot_index * rows_own, rows_own, 1)
    intra_rates = fit_rates(intra_share, row_counts, patch_counts, shot_total)
    load_share = jnp.sum(intra_rates, axis=2)
    detector_load = gather_directly(load_share, "det", 0)
    pair_slot, valid = route_table(pair_owners[0].reshape(-1), shot_count, recv_slots)
    fitted = fit_rates(
        pair_share,
        jnp.take(row_counts, pair_ends[:, 0], axis=0),
        jnp.take(patch_counts, pair_ends[:, 1], axis=0),
        shot_total,
    )
    outgoing = jnp.take(fitted, pair_slot.reshape(-1), axis=0).reshape(
        shot_count, recv_slots, rows_own, PB
    )
    outgoing = outgoing * valid[:, :, None, None]
    incoming = lax.all_to_all(outgoing, SHOT, split_axis=0, concat_axis=2, tiled=True)
    boundary = incoming.reshape(recv_slots, PB, PB)
    moments = triple_total * inverse
    means = jnp.take(counts, triple_index.reshape(-1), axis=0).reshape(triple_count, 3) * inverse
    mean_first = means[:, 0]
    mean_second = means[:, 1]
    mean_third = means[:, 2]
    kappa = (
        moments[3]
        - moments[0] * mean_third
        - moments[1] * mean_second
        - moments[2] * mean_first
        + 2.0 * mean_first * mean_second * mean_third
    )
    triple_cumulant = 1000.0 * kappa
    return (intra_rates, boundary[None, None], detector_load, triple_cumulant[None])


def solution(mesh):
    torus = Mesh(
        mesh.devices.reshape(4, 8, 2, mesh.shape["det"]), ("shot_0", "shot_1", "shot_2", "det")
    )
    return jax.shard_map(
        local,
        mesh=torus,
        in_specs=(P(SHOT, "det"), P("det", None, None), P("det", None, None), P("det", None, None)),
        out_specs=(
            P("det", SHOT, None),
            P("det", SHOT, None, None, None),
            P(None, SHOT),
            P("det", None),
        ),
        check_vma=False,
    )
```

profile of v0, /device:TPU:1, one launch (start us, length us, event | category | flops | bytes accessed | tf_op | source)
XLA Modules:
  0.0 155.3 jit_solution(5718766093984803097)
XLA Ops:
  0.6 5.4 %copy.90 = s32[1024,1024]{0,1:T(8,128)} copy(s32[1024,1024]{1,0:T(8,128)} %param.6) | data formatting | bytes 8388608 | tf_op args[0]
  6.0 2.8 %convert_element_type.24 = bf16[1024,1024]{0,1:T(8,128)(2,1)S(1)} convert(s32[1024,1024]{0,1:T(8,128)} %copy.90) | non-fusion elementwise | flops 1048576 | bytes 6291456 | tf_op jit(solution)/shard_map/convert_element_type | solution.py:76
  8.8 1.3 copy-done
  10.1 0.7 fusion.24
  10.8 3.0 %copy.92 = bf16[1024,8,128]{2,0,1:T(8,128)(2,1)S(1)} copy(bf16[1024,8,128]{0,2,1:T(8,128)(2,1)} %bitcast.87) | data formatting | bytes 4194304 | tf_op jit(solution)/shard_map/reshape | solution.py:77
  13.9 4.5 %gather_fusion.6 = bf16[26,1024,128]{2,1,0:T(8,128)(2,1)} fusion(bf16[1024,8,128]{2,0,1:T(8,128)(2,1)S(1)} %copy.92, s32[1024]{0:T(1024)S(1)} %get-tuple-element.40), kind=kCustom, calls=%fused_computation.1.clone | custom fusion | bytes 13631592 | tf_op jit(solution)/shard_map/jit(_take)/gather | solution.py:99
  18.5 4.6 %gather_fusion.5 = bf16[26,1024,128]{2,1,0:T(8,128)(2,1)} fusion(bf16[1024,8,128]{2,0,1:T(8,128)(2,1)S(1)} %copy.92, s32[1024]{0:T(1024)S(1)} %get-tuple-element.41), kind=kCustom, calls=%fused_computation.clone | custom fusion | bytes 13631592 | tf_op jit(solution)/shard_map/jit(_take)/gather | solution.py:98
  23.1 7.4 %fusion = f32[26,128,128]{2,1,0:T(8,128)S(1)} fusion(bf16[26,1024,128]{2,1,0:T(8,128)(2,1)} %gather_fusion.6, bf16[26,1024,128]{2,1,0:T(8,128)(2,1)} %gather_fusion.5, pred[26]{0:T(512)(128)(4,1)S(1)} %get-tuple-element.36, pred[26]{0:T(512)(128)(4,1)S(1)} %get-tuple-element.22), kind=kOutput, calls=%fused_computation.7 | convolution fusion | flops 879230976 | bytes 15335476 | tf_op jit(solution)/shard_map/spi,spj->pij/dot_general | solution.py:100
  30.5 0.1 pad_maximum_fusion
  30.7 2.1 %copy.115 = f32[34,64,2,128]{3,2,0,1:T(2,128)} copy(f32[34,64,2,128]{3,2,1,0:T(2,128)S(1)} %bitcast.89) | data formatting | bytes 4456448 | tf_op jit(solution)/shard_map/reshape | solution.py:13
  32.8 11.8 %all-to-all-start = ((f32[64,34,2,128]{3,2,1,0:T(2,128)}), f32[64,34,2,128]{3,2,1,0:T(2,128)}, u32[]{:S(2)}, u32[]{:S(2)}) async-start(f32[64,34,2,128]{3,2,1,0:T(2,128)} %bitcast.83), calls=%async_computation | async-start | bytes 4456448 | tf_op jit(solution)/shard_map/all_to_all | solution.py:18
  44.6 2.5 %reduce_sum.73 = s32[1024]{0:T(1024)S(1)} reduce(s32[1024,1024]{1,0:T(8,128)} %param.6, s32[]{:T(128)} %constant.84.clone.1), dimensions={0}, to_apply=%region_1.0 | reduce | flops 1047552 | bytes 4198404 | tf_op jit(solution)/shard_map/reduce_sum | solution.py:78
  47.1 0.1 copy.96
  47.2 0.1 eq.36
  47.4 0.1 copy.97
  47.5 0.2 reduce_window_sum.11
  47.9 0.1 copy.101
  48.0 0.1 copy.100
  48.2 0.1 reshape.306
  48.3 0.1 copy.102
  48.4 0.1 copy.106
  48.5 0.2 reshape_squeeze.7
  48.9 6.1 %gather_fusion.3 = s32[768,1024]{1,0:T(8,128)S(1)} fusion(s32[1024,1024]{0,1:T(8,128)} %copy.90, s32[1024]{0:T(1024)S(1)} %pad_clamp_fusion), kind=kCustom, calls=%fused_computation.5 | custom fusion | bytes 6294528 | tf_op jit(solution)/shard_map/jit(_take)/gather | solution.py:81
  55.1 3.1 %gather.34 = s32[1024,256,3]{0,2,1:T(4,128)} reshape(s32[1024,768]{0,1:T(8,128)S(1)} %bitcast.88) | data formatting | bytes 6291456 | tf_op jit(solution)/shard_map/jit(_take)/gather | solution.py:81
  58.2 3.4 %copy.110 = s32[1024,256,3]{1,0,2:T(8,128)S(1)} copy(s32[1024,256,3]{0,2,1:T(4,128)} %gather.34) | data formatting | bytes 6291456 | tf_op jit(solution)/shard_map/jit(_take)/gather | solution.py:81
  61.6 0.3 select_convert_fusion
  61.9 0.3 fusion.9
  62.2 9.9 %all-reduce.1 = (f32[1024]{0:T(1024)S(1)}, f32[4,256]{1,0:T(4,128)S(1)}) all-reduce(f32[1024]{0:T(1024)S(1)} %convert_element_type.25, f32[4,256]{1,0:T(4,128)S(1)} %pad_maximum_fusion.1), channel_id=1, replica_groups=mesh['shot_0'=4,'shot_1'=8,'shot_2'=2,'det'=8] {'shot_0'}, use_global_device_ids=true, to_apply=%region_2.4 | all-reduce | flops 2048 | bytes 16384 | tf_op jit(solution)/shard_map/psum | solution.py:24
  72.2 30.8 %all-reduce = (f32[1024]{0:T(1024)S(1)}, f32[4,256]{1,0:T(4,128)S(1)}) all-reduce(f32[1024]{0:T(1024)S(1)} %get-tuple-element.14, f32[4,256]{1,0:T(4,128)S(1)} %get-tuple-element.15), channel_id=1, replica_groups=mesh['shot_0'=4,'shot_1'=8,'shot_2'=2,'det'=8] {'shot_1'}, use_global_device_ids=true, to_apply=%region_3.5 | all-reduce | flops 2048 | bytes 16384 | tf_op jit(solution)/shard_map/psum | solution.py:24
  103.0 5.2 %all-reduce.2 = (f32[1024]{0:T(1024)S(1)}, f32[4,256]{1,0:T(4,128)S(1)}) all-reduce(f32[1024]{0:T(1024)S(1)} %get-tuple-element.12, f32[4,256]{1,0:T(4,128)S(1)} %get-tuple-element.13), channel_id=1, replica_groups=mesh['shot_0'=4,'shot_1'=8,'shot_2'=2,'det'=8] {'shot_2'}, use_global_device_ids=true, to_apply=%region_4.6 | all-reduce | flops 2048 | bytes 16384 | tf_op jit(solution)/shard_map/psum | solution.py:24
  108.2 3.2 %gather_fusion.4 = f32[768]{0:T(1024)S(1)} fusion(f32[1024]{0:T(1024)S(1)} %get-tuple-element.16, s32[1024]{0:T(1024)S(1)} %pad_clamp_fusion), kind=kCustom, calls=%fused_computation.6 | custom fusion | bytes 9216 | tf_op jit(solution)/shard_map/jit(_take)/gather | solution.py:126
  111.4 0.2 gather.36
  111.6 0.6 gather_fusion.1
  112.3 0.6 gather_fusion
  113.1 2.3 %reduce_sum.72 = f32[34,2,128]{2,1,0:T(2,128)S(1)} reduce(f32[64,34,2,128]{3,2,1,0:T(2,128)} %all-to-all-done, f32[]{:T(128)} %constant.82.clone.1), dimensions={0}, to_apply=%region_0.2 | reduce | flops 548352 | bytes 2263044 | tf_op jit(solution)/shard_map/reduce_sum | solution.py:19
  115.4 0.7 fusion.23
  116.2 0.6 broadcast_in_dim.91
  116.8 10.0 %all-to-all-start.2 = ((f32[8,8,2]{1,2,0:T(2,128)}), f32[8,8,2]{1,2,0:T(2,128)S(1)}, u32[]{:S(2)}, u32[]{:S(2)}) async-start(f32[8,8,2]{1,2,0:T(2,128)} %broadcast_in_dim.91), calls=%async_computation.2 | async-start | bytes 16384 | tf_op jit(solution)/shard_map/all_to_all | solution.py:36
  126.7 0.2 subtract_multiply_fusion
  126.9 0.7 gather_fusion.2
  127.7 1.0 select_multiply_fusion.1
  128.7 4.7 %all-to-all-done.2 = f32[8,8,2]{1,2,0:T(2,128)S(1)} async-done(((f32[8,8,2]{1,2,0:T(2,128)}), f32[8,8,2]{1,2,0:T(2,128)S(1)}, u32[]{:S(2)}, u32[]{:S(2)}) %all-to-all-start.2) | async-done | bytes 544 | tf_op jit(solution)/shard_map/all_to_all | solution.py:36
  133.3 11.0 %all-to-all-start.1 = ((f32[64,2,2,128]{3,2,1,0:T(2,128)}), f32[64,2,2,128]{3,2,1,0:T(2,128)S(1)}, u32[]{:S(2)}, u32[]{:S(2)}) async-start(f32[64,2,2,128]{3,2,1,0:T(2,128)} %select_multiply_fusion.1), calls=%async_computation.1 | async-start | bytes 262144 | tf_op jit(solution)/shard_map/all_to_all | solution.py:123
  144.3 0.3 slice_reduce_fusion
  144.6 0.6 fusion.17
  145.1 0.6 reshape.307
  145.8 8.8 %all-to-all-done.1 = f32[64,2,2,128]{3,2,1,0:T(2,128)S(1)} async-done(((f32[64,2,2,128]{3,2,1,0:T(2,128)}), f32[64,2,2,128]{3,2,1,0:T(2,128)S(1)}, u32[]{:S(2)}, u32[]{:S(2)}) %all-to-all-start.1) | async-done | bytes 131104 | tf_op jit(solution)/shard_map/all_to_all | solution.py:123
  154.6 0.7 copy.103
  (39 shorter events, 0.9 us)
Async XLA Ops:
  8.8 1.4 copy-start
  10.8 3.1 %copy-start.1 = (s32[1,26,2]{1,2,0:T(2,128)S(1)}, s32[1,26,2]{1,2,0:T(2,128)}, u32[]{:S(2)}) copy-start(s32[1,26,2]{1,2,0:T(2,128)} %param.7) | copy-start | bytes 628
  32.8 80.3 %all-to-all-start = ((f32[64,34,2,128]{3,2,1,0:T(2,128)}), f32[64,34,2,128]{3,2,1,0:T(2,128)}, u32[]{:S(2)}, u32[]{:S(2)}) async-start(f32[64,34,2,128]{3,2,1,0:T(2,128)} %bitcast.83), calls=%async_computation | async-start | bytes 4456448 | tf_op jit(solution)/shard_map/all_to_all | solution.py:18
  44.6 2.5 %copy-start.3 = (s32[1,26,2]{1,2,0:T(2,128)S(1)}, s32[1,26,2]{1,2,0:T(2,128)}, u32[]{:S(2)}) copy-start(s32[1,26,2]{1,2,0:T(2,128)} %param.8) | copy-start | bytes 628
  44.6 3.8 %copy-start.2 = (s32[1,256,3]{1,0,2:T(1,128)S(1)}, s32[1,256,3]{1,0,2:T(1,128)}, u32[]{:S(2)}) copy-start(s32[1,256,3]{1,0,2:T(1,128)} %param.9) | copy-start | bytes 9220
  116.8 16.6 %all-to-all-start.2 = ((f32[8,8,2]{1,2,0:T(2,128)}), f32[8,8,2]{1,2,0:T(2,128)S(1)}, u32[]{:S(2)}, u32[]{:S(2)}) async-start(f32[8,8,2]{1,2,0:T(2,128)} %broadcast_in_dim.91), calls=%async_computation.2 | async-start | bytes 16384 | tf_op jit(solution)/shard_map/all_to_all | solution.py:36
  133.3 21.3 %all-to-all-start.1 = ((f32[64,2,2,128]{3,2,1,0:T(2,128)}), f32[64,2,2,128]{3,2,1,0:T(2,128)S(1)}, u32[]{:S(2)}, u32[]{:S(2)}) async-start(f32[64,2,2,128]{3,2,1,0:T(2,128)} %select_multiply_fusion.1), calls=%async_computation.1 | async-start | bytes 262144 | tf_op jit(solution)/shard_map/all_to_all | solution.py:123
where the time goes:
time: 156 us; the launch traced here: 155 us
  blocking collectives  45.9 us (29%)
  local copies, waits for them, and re-layouts  42.5 us (27%)
  starting transfers between devices  32.7 us (21%)
  waiting for transfers between devices  13.5 us (9%)
  other arithmetic  11.5 us (7%)
  matrix products  8.12 us (5%)
    psum x3, blocking collectives, by_axis(): x = lax.psum(x, axis)  45.9 us
    gather x3, local copies, waits for them, and re-layouts, local(): jnp.take(events, triple_index.reshape(-1), axis=1).astype(jnp.float32)  12.6 us
    all_to_all x1, starting transfers between devices, sum_at_owner(): lax.all_to_all(tiles, axis, split_axis=0, concat_axis=0, tiled=True)  11.8 us
    all_to_all x1, starting transfers between devices, local(): lax.all_to_all(outgoing, SHOT, split_axis=0, concat_axis=2, tiled=True)  11 us
    all_to_all x1, starting transfers between devices, sent_to_all(): return lax.all_to_all(copies, axis, split_axis=0, concat_axis=0, tiled=True)  9.97 us
    all_to_all x1, waiting for transfers between devices, local(): lax.all_to_all(outgoing, SHOT, split_axis=0, concat_axis=2, tiled=True)  8.84 us
    dot_general x1, matrix products, local(): jnp.einsum('spi,spj->pij', first_columns, second_columns, preferred_eleme...  7.41 us
    unnamed x11, local copies, waits for them, and re-layouts  6.97 us
  transfers between devices with their start and end apart: 3, of which 2 were waited for; matrix products, arithmetic and copies ran while one was open for 17% of the time, Pallas kernels for 0%

commit v1 on v0

--- a/solution.py
+++ b/solution.py
@@ -21,7 +21,7 @@
 
 def by_axis(x, axes):
     for axis in axes:
-        x = lax.psum(x, axis)
+        x = jnp.sum(lax.all_gather(x, axis), axis=0)
     return x
 
 

time: 156 us -> 219 us (1.40)
  blocking collectives: 45.9 us -> 108 us
    all_gather x0 -> x6, blocking collectives: none -> 108 us  [by_axis(): x = jnp.sum(lax.all_gather(x, axis), axis=0)]
    psum x3 -> x0, blocking collectives: 45.9 us -> none  [by_axis(): x = lax.psum(x, axis)]
    unnamed x11 -> x15, local copies, waits for them, and re-layouts: 6.97 us -> 6.98 us
  transfers between devices with their start and end apart: 3 -> 3, of which waited for: 2 -> 2; matrix products, arithmetic and copies ran while one was open for 17% -> 13% of each run, Pallas kernels for 0% -> 0%
where the time goes in v1:
time: 219 us
  blocking collectives  108 us (49%)
  local copies, waits for them, and re-layouts  44.5 us (20%)
  starting transfers between devices  31.4 us (14%)
  waiting for transfers between devices  13.5 us (6%)
  other arithmetic  12.1 us (6%)
  matrix products  8.12 us (4%)
    all_gather x6, blocking collectives, by_axis(): x = jnp.sum(lax.all_gather(x, axis), axis=0)  108 us
    gather x3, local copies, waits for them, and re-layouts, local(): jnp.take(events, triple_index.reshape(-1), axis=1).astype(jnp.float32)  12.6 us
    all_to_all x1, starting transfers between devices, sum_at_owner(): lax.all_to_all(tiles, axis, split_axis=0, concat_axis=0, tiled=True)  11.8 us
    all_to_all x1, starting transfers between devices, sent_to_all(): return lax.all_to_all(copies, axis, split_axis=0, concat_axis=0, tiled=True)  9.94 us
    all_to_all x1, starting transfers between devices, local(): lax.all_to_all(outgoing, SHOT, split_axis=0, concat_axis=2, tiled=True)  9.73 us
    all_to_all x1, waiting for transfers between devices, local(): lax.all_to_all(outgoing, SHOT, split_axis=0, concat_axis=2, tiled=True)  8.84 us
    dot_general x1, matrix products, local(): jnp.einsum('spi,spj->pij', first_columns, second_columns, preferred_eleme...  7.41 us
    unnamed x15, local copies, waits for them, and re-layouts  6.98 us
  transfers between devices with their start and end apart: 3, of which 2 were waited for; matrix products, arithmetic and copies ran while one was open for 13% of the time, Pallas kernels for 0%

profile of v1, /device:TPU:1, one launch (start us, length us, event | category | flops | bytes accessed | tf_op | source)
XLA Modules:
  0.0 218.5 jit_solution(3087502450818276889)
XLA Ops:
  0.6 5.4 %copy.90 = s32[1024,1024]{0,1:T(8,128)} copy(s32[1024,1024]{1,0:T(8,128)} %param.6) | data formatting | bytes 8388608 | tf_op args[0]
  6.0 2.8 %convert_element_type.34 = bf16[1024,1024]{0,1:T(8,128)(2,1)S(1)} convert(s32[1024,1024]{0,1:T(8,128)} %copy.90) | non-fusion elementwise | flops 1048576 | bytes 6291456 | tf_op jit(solution)/shard_map/convert_element_type | solution.py:76
  8.8 1.3 copy-done
  10.1 0.7 fusion.24
  10.8 3.0 %copy.92 = bf16[1024,8,128]{2,0,1:T(8,128)(2,1)S(1)} copy(bf16[1024,8,128]{0,2,1:T(8,128)(2,1)} %bitcast.90) | data formatting | bytes 4194304 | tf_op jit(solution)/shard_map/reshape | solution.py:77
  13.9 4.5 %gather_fusion.6 = bf16[26,1024,128]{2,1,0:T(8,128)(2,1)} fusion(bf16[1024,8,128]{2,0,1:T(8,128)(2,1)S(1)} %copy.92, s32[1024]{0:T(1024)S(1)} %get-tuple-element.36), kind=kCustom, calls=%fused_computation.1.clone | custom fusion | bytes 13631592 | tf_op jit(solution)/shard_map/jit(_take)/gather | solution.py:99
  18.5 4.6 %gather_fusion.5 = bf16[26,1024,128]{2,1,0:T(8,128)(2,1)} fusion(bf16[1024,8,128]{2,0,1:T(8,128)(2,1)S(1)} %copy.92, s32[1024]{0:T(1024)S(1)} %get-tuple-element.37), kind=kCustom, calls=%fused_computation.clone | custom fusion | bytes 13631592 | tf_op jit(solution)/shard_map/jit(_take)/gather | solution.py:98
  23.1 7.4 %fusion = f32[26,128,128]{2,1,0:T(8,128)S(1)} fusion(bf16[26,1024,128]{2,1,0:T(8,128)(2,1)} %gather_fusion.6, bf16[26,1024,128]{2,1,0:T(8,128)(2,1)} %gather_fusion.5, pred[26]{0:T(512)(128)(4,1)S(1)} %get-tuple-element.32, pred[26]{0:T(512)(128)(4,1)S(1)} %get-tuple-element.18), kind=kOutput, calls=%fused_computation.7 | convolution fusion | flops 879230976 | bytes 15335476 | tf_op jit(solution)/shard_map/spi,spj->pij/dot_general | solution.py:100
  30.5 0.1 pad_maximum_fusion
  30.7 2.1 copy.115
  32.8 11.8 %all-to-all-start = ((f32[64,34,2,128]{3,2,1,0:T(2,128)}), f32[64,34,2,128]{3,2,1,0:T(2,128)}, u32[]{:S(2)}, u32[]{:S(2)}) async-start(f32[64,34,2,128]{3,2,1,0:T(2,128)} %bitcast.86), calls=%async_computation | async-start | bytes 4456448 | tf_op jit(solution)/shard_map/all_to_all | solution.py:18
  44.6 2.5 %reduce_sum.127 = s32[1024]{0:T(1024)S(1)} reduce(s32[1024,1024]{1,0:T(8,128)} %param.6, s32[]{:T(128)} %constant.84.clone.1), dimensions={0}, to_apply=%region_1.0 | reduce | flops 1047552 | bytes 4198404 | tf_op jit(solution)/shard_map/reduce_sum | solution.py:78
  47.1 10.9 %all-gather = f32[4096]{0:T(1024)S(1)} all-gather(f32[1024]{0:T(1024)S(1)} %convert_element_type.35), channel_id=2, replica_groups=mesh['shot_0'=4,'shot_1'=8,'shot_2'=2,'det'=8] {'shot_0'}, dimensions={0}, use_global_device_ids=true | all-gather | bytes 20480 | tf_op jit(solution)/shard_map/all_gather | solution.py:24
  58.2 50.4 %all-gather.1 = f32[8192]{0:T(1024)S(1)} all-gather(f32[1024]{0:T(1024)S(1)} %reduce_sum.128), channel_id=3, replica_groups=mesh['shot_0'=4,'shot_1'=8,'shot_2'=2,'det'=8] {'shot_1'}, dimensions={0}, use_global_device_ids=true | all-gather | bytes 36864 | tf_op jit(solution)/shard_map/all_gather | solution.py:24
  108.6 7.6 %all-gather.2 = f32[2048]{0:T(1024)S(1)} all-gather(f32[1024]{0:T(1024)S(1)} %reduce_sum.129), channel_id=4, replica_groups=mesh['shot_0'=4,'shot_1'=8,'shot_2'=2,'det'=8] {'shot_2'}, dimensions={0}, use_global_device_ids=true | all-gather | bytes 12288 | tf_op jit(solution)/shard_map/all_gather | solution.py:24
  116.3 0.2 reduce_window_sum.11
  117.0 0.7 reshape.314
  117.7 0.7 copy.102
  118.4 0.1 copy.106
  118.5 0.2 reshape_squeeze.7
  118.8 6.1 %gather_fusion.3 = s32[768,1024]{1,0:T(8,128)S(1)} fusion(s32[1024,1024]{0,1:T(8,128)} %copy.90, s32[1024]{0:T(1024)S(1)} %pad_clamp_fusion), kind=kCustom, calls=%fused_computation.5 | custom fusion | bytes 6294528 | tf_op jit(solution)/shard_map/jit(_take)/gather | solution.py:81
  125.0 3.2 %gather_fusion.4 = f32[768]{0:T(1024)S(1)} fusion(f32[1024]{0:T(1024)S(1)} %reduce_sum.130, s32[1024]{0:T(1024)S(1)} %pad_clamp_fusion), kind=kCustom, calls=%fused_computation.6 | custom fusion | bytes 9216 | tf_op jit(solution)/shard_map/jit(_take)/gather | solution.py:126
  128.2 0.2 gather.36
  128.4 0.6 select_multiply_fusion
  129.0 0.8 copy.107
  129.8 3.1 %gather.34 = s32[1024,256,3]{0,2,1:T(4,128)} reshape(s32[1024,768]{0,1:T(8,128)S(1)} %bitcast.91) | data formatting | bytes 6291456 | tf_op jit(solution)/shard_map/jit(_take)/gather | solution.py:81
  132.9 3.4 %copy.110 = s32[1024,256,3]{1,0,2:T(8,128)S(1)} copy(s32[1024,256,3]{0,2,1:T(4,128)} %gather.34) | data formatting | bytes 6291456 | tf_op jit(solution)/shard_map/jit(_take)/gather | solution.py:81
  136.3 0.2 select_convert_fusion
  136.6 0.3 fusion.9
  136.9 9.8 %all-gather.6 = f32[4,4,256]{2,1,0:T(4,128)S(1)} all-gather(f32[1,4,256]{2,1,0:T(4,128)S(1)} %maximum_bitcast_fusion), channel_id=5, replica_groups=mesh['shot_0'=4,'shot_1'=8,'shot_2'=2,'det'=8] {'shot_0'}, dimensions={0}, use_global_device_ids=true | all-gather | bytes 20480 | tf_op jit(solution)/shard_map/all_gather | solution.py:24
  146.7 18.3 %all-gather.7 = f32[8,4,256]{2,1,0:T(4,128)S(1)} all-gather(f32[1,4,256]{2,1,0:T(4,128)S(1)} %bitcast.97), channel_id=6, replica_groups=mesh['shot_0'=4,'shot_1'=8,'shot_2'=2,'det'=8] {'shot_1'}, dimensions={0}, use_global_device_ids=true | all-gather | bytes 36864 | tf_op jit(solution)/shard_map/all_gather | solution.py:24
  165.0 11.1 %all-gather.8 = f32[2,4,256]{2,1,0:T(4,128)S(1)} all-gather(f32[1,4,256]{2,1,0:T(4,128)S(1)} %bitcast.96), channel_id=7, replica_groups=mesh['shot_0'=4,'shot_1'=8,'shot_2'=2,'det'=8] {'shot_2'}, dimensions={0}, use_global_device_ids=true | all-gather | bytes 12288 | tf_op jit(solution)/shard_map/all_gather | solution.py:24
  176.1 0.6 gather_fusion.1
  176.7 0.6 gather_fusion
  177.6 2.3 %reduce_sum.126 = f32[34,2,128]{2,1,0:T(2,128)S(1)} reduce(f32[64,34,2,128]{3,2,1,0:T(2,128)} %all-to-all-done, f32[]{:T(128)} %constant.82.clone.1), dimensions={0}, to_apply=%region_0.2 | reduce | flops 548352 | bytes 2263044 | tf_op jit(solution)/shard_map/reduce_sum | solution.py:19
  179.8 0.7 fusion.23
  180.6 0.6 broadcast_in_dim.91
  181.2 9.9 %all-to-all-start.2 = ((f32[8,8,2]{1,2,0:T(2,128)}), f32[8,8,2]{1,2,0:T(2,128)S(1)}, u32[]{:S(2)}, u32[]{:S(2)}) async-start(f32[8,8,2]{1,2,0:T(2,128)} %broadcast_in_dim.91), calls=%async_computation.2 | async-start | bytes 16384 | tf_op jit(solution)/shard_map/all_to_all | solution.py:36
  191.2 0.2 subtract_multiply_fusion
  191.3 0.7 gather_fusion.2
  192.1 1.0 select_multiply_fusion.1
  193.1 4.7 %all-to-all-done.2 = f32[8,8,2]{1,2,0:T(2,128)S(1)} async-done(((f32[8,8,2]{1,2,0:T(2,128)}), f32[8,8,2]{1,2,0:T(2,128)S(1)}, u32[]{:S(2)}, u32[]{:S(2)}) %all-to-all-start.2) | async-done | bytes 544 | tf_op jit(solution)/shard_map/all_to_all | solution.py:36
  197.7 9.7 %all-to-all-start.1 = ((f32[64,2,2,128]{3,2,1,0:T(2,128)}), f32[64,2,2,128]{3,2,1,0:T(2,128)S(1)}, u32[]{:S(2)}, u32[]{:S(2)}) async-start(f32[64,2,2,128]{3,2,1,0:T(2,128)} %select_multiply_fusion.1), calls=%async_computation.1 | async-start | bytes 262144 | tf_op jit(solution)/shard_map/all_to_all | solution.py:123
  207.5 0.3 slice_reduce_fusion
  207.7 0.6 fusion.17
  208.3 0.6 reshape.315
  209.0 8.8 %all-to-all-done.1 = f32[64,2,2,128]{3,2,1,0:T(2,128)S(1)} async-done(((f32[64,2,2,128]{3,2,1,0:T(2,128)}), f32[64,2,2,128]{3,2,1,0:T(2,128)S(1)}, u32[]{:S(2)}, u32[]{:S(2)}) %all-to-all-start.1) | async-done | bytes 131104 | tf_op jit(solution)/shard_map/all_to_all | solution.py:123
  217.8 0.7 copy.103
  (53 shorter events, 1.4 us)
Async XLA Ops:
  8.8 1.4 copy-start
  10.8 3.1 %copy-start.2 = (s32[1,26,2]{1,2,0:T(2,128)S(1)}, s32[1,26,2]{1,2,0:T(2,128)}, u32[]{:S(2)}) copy-start(s32[1,26,2]{1,2,0:T(2,128)} %param.7) | copy-start | bytes 628
  32.8 144.7 %all-to-all-start = ((f32[64,34,2,128]{3,2,1,0:T(2,128)}), f32[64,34,2,128]{3,2,1,0:T(2,128)}, u32[]{:S(2)}, u32[]{:S(2)}) async-start(f32[64,34,2,128]{3,2,1,0:T(2,128)} %bitcast.86), calls=%async_computation | async-start | bytes 4456448 | tf_op jit(solution)/shard_map/all_to_all | solution.py:18
  44.6 13.4 %copy-start.4 = (s32[1,26,2]{1,2,0:T(2,128)S(1)}, s32[1,26,2]{1,2,0:T(2,128)}, u32[]{:S(2)}) copy-start(s32[1,26,2]{1,2,0:T(2,128)} %param.8) | copy-start | bytes 628
  44.6 73.8 %copy-start.3 = (s32[1,256,3]{1,0,2:T(1,128)S(1)}, s32[1,256,3]{1,0,2:T(1,128)}, u32[]{:S(2)}) copy-start(s32[1,256,3]{1,0,2:T(1,128)} %param.9) | copy-start | bytes 9220
  136.6 40.7 %copy-start.5 = (s32[128,1]{0,1:T(1,128)S(1)}, s32[128,1]{0,1:T(1,128)}, u32[]{:S(2)}) copy-start(s32[128,1]{0,1:T(1,128)} %reshape.314) | copy-start | bytes 1540
  136.6 55.5 %copy-start.1 = (f32[64,2]{1,0:T(8,128)S(1)}, f32[64,2]{1,0:T(8,128)}, u32[]{:S(2)}) copy-start(f32[64,2]{1,0:T(8,128)} %copy.102) | copy-start | bytes 1540
  181.2 16.5 %all-to-all-start.2 = ((f32[8,8,2]{1,2,0:T(2,128)}), f32[8,8,2]{1,2,0:T(2,128)S(1)}, u32[]{:S(2)}, u32[]{:S(2)}) async-start(f32[8,8,2]{1,2,0:T(2,128)} %broadcast_in_dim.91), calls=%async_computation.2 | async-start | bytes 16384 | tf_op jit(solution)/shard_map/all_to_all | solution.py:36
  197.7 20.1 %all-to-all-start.1 = ((f32[64,2,2,128]{3,2,1,0:T(2,128)}), f32[64,2,2,128]{3,2,1,0:T(2,128)S(1)}, u32[]{:S(2)}, u32[]{:S(2)}) async-start(f32[64,2,2,128]{3,2,1,0:T(2,128)} %select_multiply_fusion.1), calls=%async_computation.1 | async-start | bytes 262144 | tf_op jit(solution)/shard_map/all_to_all | solution.py:123
